TPU v7x, 32 devices: a whole 2x2x4 slice. The times are simulated.
32 devices in a mesh: gx: 4 (over y, x), gy: 2 (over core), gz: 4 (over z).
Axes of the slice: x: 2, y: 2, z: 4, core: 2. Of those that a mesh axis runs over, the one named last changes fastest.
Arguments:
- conserved: float32 [5, 64, 32, 512], P(None, 'gx', 'gy', 'gz'), as said below
Outputs:
- advanced: float32 [5, 64, 32, 512], P(None, 'gx', 'gy', 'gz')
Inputs may be any that keep to these rules, and one draw needn't show every extreme that they name: `conserved`: every cell has positive density and positive pressure (energy above the kinetic energy).
All inputs are finite; a program needn't handle non-finite values. Where the computation divides by a largest or mean magnitude, that divisor is 1e-20 or more.
Results may differ from a plain program's by a relative error of at most 0.000066.
Values sent between devices are 32-bit elements; how exact they have to be, the bound alone decides.
A program may use at most 64 MiB of HBM per device.

v0:
```python
import functools

import jax
import jax.numpy as jnp
from jax import lax
from jax.experimental import pallas as pl
from jax.experimental.pallas import tpu as pltpu
from jax.sharding import PartitionSpec as P

GAMMA = 1.4
EPS = 1e-06
COURANT = 0.4
K13 = 13.0 / 3.0
MESH = pl.DeviceIdType.MESH
AXES = ("gx", "gy", "gz")
ORDERS = ([0, 1, 2, 3, 4], [0, 2, 1, 3, 4], [0, 3, 1, 2, 4])
LANES = 128


def project(u, vn, va, vb, kin, b1h, ich):
    a = u[4] + kin * u[0] - vn * u[1] - va * u[2] - vb * u[3]
    a = b1h * a
    b = (vn * u[0] - u[1]) * ich
    return [a + b, u[2] - va * u[0], u[3] - vb * u[0], u[0] - (a + a), a - b]


def nonlinear(e1, e2, e3, f0, f1):
    f2 = e3 - (f1 + e2)
    q0 = 1.0 / ((K13 * (e1 * e1) + EPS) + f0 * f0)
    q1 = 1.0 / ((K13 * (e2 * e2) + EPS) + f1 * f1)
    q2 = 1.0 / ((K13 * (e3 * e3) + EPS) + f2 * f2)
    w0 = q0 * q0
    w2 = 3.0 * (q2 * q2)
    n0 = e1 - e2
    return (w0 * (n0 + n0) + w2 * (e2 - e3)) / (w0 + w2 + 6.0 * (q1 * q1))


def flux_sweep(direction, slots, lane_rows, quarter, q, p, m, f6, ep, em, hp, hm, flux):
    order = ORDERS[direction]

    def at(ref, c, j):
        return ref[c, pl.ds(pl.multiple_of(8 * j, 8), 8), :]

    def put(ref, c, j, value):
        ref[c, pl.ds(pl.multiple_of(8 * j, 8), 8), :] = value

    r = lane_rows

    def cell(j, _):
        s = [at(q, order[c], j) for c in range(5)]
        inv = 1.0 / s[0]
        vq = s[1] * (0.25 * inv)
        pq = 0.25 * (GAMMA - 1.0) * (s[4] - (0.5 * inv) * (s[1] * s[1] + s[2] * s[2] + s[3] * s[3]))
        f = [0.25 * s[1], s[1] * vq + pq, s[2] * vq, s[3] * vq, s[4] * vq + 4.0 * (pq * vq)]
        for c in range(5):
            sq = quarter * s[c]
            put(p, c, j, f[c] + sq)
            put(m, c, j, f[c] - sq)
            put(f6, c, j, 6.0 * f[c])
        return 0

    lax.fori_loop(0, (slots + 6) * r, cell, 0, unroll=2)

    def differ(i, _):
        j = i + r
        for c in range(5):
            for src, e, h in ((p, ep, hp), (m, em, hm)):
                low, mid, high = at(src, c, j - r), at(src, c, j), at(src, c, j + r)
                below = mid - low
                put(e, c, j, (high - mid) - below)
                put(h, c, j, below + below)
        return 0

    lax.fori_loop(0, (slots + 4) * r, differ, 0, unroll=2)

    def face(j, _):
        mean = [at(q, order[c], j + 2 * r) + at(q, order[c], j + 3 * r) for c in range(5)]
        inv = 1.0 / mean[0]
        vn, va, vb = mean[1] * inv, mean[2] * inv, mean[3] * inv
        kin = 0.5 * (vn * vn + va * va + vb * vb)
        c2 = GAMMA * (GAMMA - 1.0) * (mean[4] * inv - kin)
        ic = lax.rsqrt(c2)
        b1h = (0.5 * (GAMMA - 1.0)) * (ic * ic)
        ich = 0.5 * ic
        args = (vn, va, vb, kin, b1h, ich)
        e2p = [at(ep, c, j + 2 * r) for c in range(5)]
        e1, e3 = ([at(ep, c, j + k * r) for c in range(5)] for k in (1, 3))
        h = [at(hp, c, j + 2 * r) for c in range(5)]
        e1, e2, e3, h = (project(u, *args) for u in (e1, e2p, e3, h))
        n = [nonlinear(e1[k], e2[k], e3[k], h[k] + e1[k], h[k] + e2[k]) for k in range(5)]
        e2m = [at(em, c, j + 3 * r) for c in range(5)]
        e1, e3 = ([at(em, c, j + k * r) for c in range(5)] for k in (4, 2))
        h = [at(hm, c, j + 4 * r) for c in range(5)]
        e1, e2, e3, h = (project(u, *args) for u in (e1, e2m, e3, h))
        n = [n[k] + nonlinear(e1[k], e2[k], e3[k], e1[k] - h[k], e2[k] - h[k]) for k in range(5)]
        d = (c2 * ic) * (n[4] - n[0])
        s15 = n[0] + n[4]
        s = s15 + n[3]
        enthalpy = (1.0 / (GAMMA - 1.0)) * c2 + kin
        out = [
            s,
            vn * s + d,
            va * s + n[1],
            vb * s + n[2],
            enthalpy * s15 + vn * d + va * n[1] + vb * n[2] + kin * n[3],
        ]
        for c in range(5):
            linear = at(f6, c, j + 2 * r) + at(f6, c, j + 3 * r)
            linear = linear - at(ep, c, j + 2 * r) - at(em, c, j + 3 * r)
            put(flux, order[c], j, linear + out[c])
        return 0

    lax.fori_loop(0, (slots + 1) * r, face, 0)


def section_kernel(
    sizes, cells, shape, cons_hbm, out_hbm, cons, out, qx, qy, qz, xh, yh, zh, ysend, zsend, mine, theirs,
    p, m, f6, ep, em, hp, hm, fx, fy, fz, halo_send, halo_recv, max_send, max_recv, load_sem, store_sem,
):
    lx, ly, lz = shape
    rows = lx * ly
    groups = rows // LANES
    blocks = 8 // groups
    inner = lz // blocks
    load = pltpu.make_async_copy(cons_hbm, cons, load_sem)
    load.start()
    peers = []
    for axis, size in zip(AXES, sizes):
        me = lax.axis_index(axis)
        peers.append([{axis: lax.rem(me + k, size)} for k in range(1, size)])
    barrier = pltpu.get_barrier_semaphore()
    count = 0
    for axis_peers in peers:
        for peer in axis_peers:
            pl.semaphore_signal(barrier, inc=1, device_id=peer, device_id_type=MESH)
            count += 1
    load.wait()

    best = [None] * 3
    for j in range(rows // 8):
        q = [cons[c, pl.ds(8 * j, 8), :] for c in range(5)]
        inv = 1.0 / q[0]
        vel = [q[d] * inv for d in (1, 2, 3)]
        kinetic = 0.5 * (vel[0] * vel[0] + vel[1] * vel[1] + vel[2] * vel[2])
        sound = jnp.sqrt((GAMMA * (GAMMA - 1.0)) * (q[4] * inv - kinetic))
        for d in range(3):
            value = jnp.abs(vel[d]) + sound
            best[d] = value if best[d] is None else jnp.maximum(best[d], value)
    for d in range(3):
        mine[0, pl.ds(d, 1), :] = jnp.max(best[d], axis=0, keepdims=True)
    mine[0, pl.ds(3, 5), :] = jnp.zeros((5, LANES), jnp.float32)

    for c in range(5):
        for k in range(3):
            ysend[0, c, pl.ds(k * lx, lx), :] = cons[c, pl.ds(ly - 3 + k, lx, stride=ly), :]
            ysend[1, c, pl.ds(k * lx, lx), :] = cons[c, pl.ds(k, lx, stride=ly), :]

    def halo(slot, src, dst, axis, size, up):
        me = lax.axis_index(axis)
        target = lax.rem(me + (1 if up else size - 1), size)
        return pltpu.make_async_remote_copy(
            src_ref=src, dst_ref=dst, send_sem=halo_send.at[slot], recv_sem=halo_recv.at[slot],
            device_id={axis: target}, device_id_type=MESH,
        )

    def spread(place, stage):
        size = sizes[stage]
        copies = []
        for k in range(size - 1):
            slot = sum(s - 1 for s in sizes[:stage]) + k
            copy = pltpu.make_async_remote_copy(
                src_ref=mine.at[place], dst_ref=theirs.at[slot],
                send_sem=max_send.at[slot], recv_sem=max_recv.at[slot],
                device_id=peers[stage][k], device_id_type=MESH,
            )
            copy.start()
            copies.append((slot, copy))
        return copies

    def gather(place, copies):
        value = mine[place]
        for slot, copy in copies:
            copy.wait_recv()
            value = jnp.maximum(value, theirs[slot])
        return value

    pl.semaphore_wait(barrier, count)
    first = spread(0, 0)
    edge = 3 * ly
    along_x = [
        halo(0, cons.at[:, pl.ds(rows - edge, edge), :], xh.at[0], "gx", sizes[0], True),
        halo(1, cons.at[:, pl.ds(0, edge), :], xh.at[1], "gx", sizes[0], False),
    ]
    along_y = [
        halo(2, ysend.at[0], yh.at[0], "gy", sizes[1], True),
        halo(3, ysend.at[1], yh.at[1], "gy", sizes[1], False),
    ]
    along_z = [
        halo(4, zsend.at[0], zh.at[0], "gz", sizes[2], True),
        halo(5, zsend.at[1], zh.at[1], "gz", sizes[2], False),
    ]
    for copy in along_y + along_x:
        copy.start()

    for c in range(5):
        for g in range(groups):
            turned = jnp.transpose(cons[c, pl.ds(g * LANES, LANES), :])
            for b in range(blocks):
                qz[c, pl.ds(24 + b * groups + g, inner, stride=8), :] = turned[b * inner:(b + 1) * inner]
            for k in range(3):
                zsend[0, c, k, g:g + 1, :] = turned[lz - 3 + k:lz - 2 + k]
                zsend[1, c, k, g:g + 1, :] = turned[k:k + 1]

    mine[1] = gather(0, first)
    second = spread(1, 2)
    for copy in along_z:
        copy.start()

    y_edge = 3 * lx
    for c in range(5):
        for y in range(ly):
            qy[c, pl.ds(y_edge + y * lx, lx), :] = cons[c, pl.ds(y, lx, stride=ly), :]

    mine[2] = gather(1, second)
    third = spread(2, 1)
    for copy in along_y:
        copy.wait()
    qy[:, pl.ds(0, y_edge), :] = yh[0]
    qy[:, pl.ds(y_edge + rows, y_edge), :] = yh[1]
    qx[:, pl.ds(edge, rows), :] = cons[...]
    top = gather(2, third)
    for _, copy in first + second + third:
        copy.wait_send()

    speeds = []
    for d in range(3):
        largest = jnp.max(top[d:d + 1], axis=1, keepdims=True)
        speeds.append(jnp.broadcast_to(largest, (8, LANES)))
    step = COURANT / (speeds[0] * cells[0] + speeds[1] * cells[1] + speeds[2] * cells[2])
    work = (p, m, f6, ep, em, hp, hm)

    flux_sweep(1, ly, lx // 8, 0.25 * speeds[1], qy, *work, fy)

    for copy in along_z:
        copy.wait()
    size = inner * 8
    for c in range(5):
        for k in range(3):
            low, high = 8 * k, 24 + size + 8 * k
            qz[c, low:low + groups, :] = zh[0, c, k]
            qz[c, low + groups:low + 8, :] = qz[c, size + 8 * k:size + 8 + 8 * k - groups, :]
            qz[c, high:high + 8 - groups, :] = qz[c, 24 + 8 * k + groups:32 + 8 * k, :]
            qz[c, high + 8 - groups:high + 8, :] = zh[1, c, k]
    flux_sweep(2, inner, 1, 0.25 * speeds[2], qz, *work, fz)

    for copy in along_x:
        copy.wait()
    qx[:, pl.ds(0, edge), :] = xh[0]
    qx[:, pl.ds(edge + rows, edge), :] = xh[1]
    flux_sweep(0, lx, ly // 8, 0.25 * speeds[0], qx, *work, fx)

    scale = [step * (cells[d] / 3.0) for d in range(3)]
    stores = []
    for c in range(5):
        def drop(j, _):
            here = pl.ds(pl.multiple_of(8 * j, 8), 8)
            fz[c, here, :] = scale[2] * (fz[c, here, :] - fz[c, pl.ds(pl.multiple_of(8 * j + 8, 8), 8), :])
            return 0

        lax.fori_loop(0, inner, drop, 0, unroll=8)
        for y in range(ly):
            for h in range(lx // 8):
                here = fy[c, pl.ds(y * lx + 8 * h, 8), :]
                there = fy[c, pl.ds((y + 1) * lx + 8 * h, 8), :]
                out[c, pl.ds(8 * h * ly + y, 8, stride=ly), :] = scale[1] * (here - there)
        for g in range(groups):
            parts = [fz[c, pl.ds(b * groups + g, inner, stride=8), :] for b in range(blocks)]
            turned = jnp.transpose(jnp.concatenate(parts, axis=0))
            for t in range(LANES // 8):
                at = g * LANES + 8 * t
                here = pl.ds(at, 8)
                change = scale[0] * (fx[c, here, :] - fx[c, pl.ds(at + ly, 8), :])
                out[c, here, :] = cons[c, here, :] + ((out[c, here, :] + change) + turned[8 * t:8 * t + 8])
        stores.append(pltpu.make_async_copy(out.at[c], out_hbm.at[c], store_sem.at[c]))
        if c > 0:
            stores[c - 1].start()
    stores[-1].start()
    for store in stores:
        store.wait()


def solution(mesh):
    sizes = [mesh.shape[axis] for axis in AXES]

    def per_device(conserved):
        _, lx, ly, lz = conserved.shape
        shape = (lx, ly, lz)
        cells = [float(n * s) for n, s in zip(shape, sizes)]
        rows = lx * ly
        groups = rows // LANES
        inner = lz * groups // 8
        assert lz == LANES and rows % LANES == 0 and 8 % groups == 0 and lx % 8 == 0 and ly % 8 == 0
        total = sum(s - 1 for s in sizes)

        def vmem(*dims):
            return pltpu.VMEM(dims, jnp.float32)

        padded = max((lx + 6) * ly, (ly + 6) * lx, (inner + 6) * 8)
        out = pl.pallas_call(
            functools.partial(section_kernel, sizes, cells, shape),
            name="section",
            out_shape=jax.ShapeDtypeStruct((5, rows, lz), jnp.float32),
            in_specs=[pl.BlockSpec(memory_space=pl.ANY)],
            out_specs=pl.BlockSpec(memory_space=pl.ANY),
            scratch_shapes=[
                vmem(5, rows, lz),
                vmem(5, rows, lz),
                vmem(5, padded, LANES),
                vmem(5, padded, LANES),
                vmem(5, padded, LANES),
                vmem(2, 5, 3 * ly, lz),
                vmem(2, 5, 3 * lx, lz),
                vmem(2, 5, 3, groups, LANES),
                vmem(2, 5, 3 * lx, lz),
                vmem(2, 5, 3, groups, LANES),
                vmem(3, 8, LANES),
                vmem(total, 8, LANES),
            ] + [vmem(5, padded, LANES)] * 7 + [
                vmem(5, (lx + 1) * ly, LANES),
                vmem(5, (ly + 1) * lx, LANES),
                vmem(5, (inner + 1) * 8, LANES),
                pltpu.SemaphoreType.DMA((6,)),
                pltpu.SemaphoreType.DMA((6,)),
                pltpu.SemaphoreType.DMA((total,)),
                pltpu.SemaphoreType.DMA((total,)),
                pltpu.SemaphoreType.DMA,
                pltpu.SemaphoreType.DMA((5,)),
            ],
            compiler_params=pltpu.CompilerParams(collective_id=0, has_side_effects=True),
        )(conserved.reshape(5, rows, lz))
        return out.reshape(conserved.shape)

    return jax.shard_map(
        per_device,
        mesh=mesh,
        in_specs=(P(None, "gx", "gy", "gz"),),
        out_specs=P(None, "gx", "gy", "gz"),
        check_vma=False,
    )
```

profile of v0, /device:TPU:0, one launch (start us, length us, event | category | flops | bytes accessed | tf_op | source)
XLA Modules:
  0.0 29.8 jit_solution(7380660098409933173)
XLA Ops:
  0.0 27.8 %section.1 = f32[5,256,128]{2,1,0:T(8,128)} custom-call(f32[5,256,128]{2,1,0:T(8,128)} %bitcast.3), custom_call_target="tpu_custom_call" | custom-call | tf_op jit(solution)/shard_map/section/pallas_call | solution.py:309
  27.9 2.0 %copy.3 = f32[5,16,16,128]{3,2,1,0:T(8,128)} copy(f32[5,16,16,128]{3,2,1,0:T(8,128)} %bitcast.2) | data formatting | bytes 1310720
where the time goes:
time: 30 us; the launch traced here: 29.8 us
  Pallas kernels  27.8 us (93%)
  local copies, waits for them, and re-layouts  1.99 us (7%)
    pallas_call x1, Pallas kernels, per_device(): pl.pallas_call(functools.partial(section_kernel, sizes, cells, shape), na...  27.8 us
    unnamed x1, local copies, waits for them, and re-layouts  1.99 us

commit v1 on v0

v1 whole, which is shorter than its diff:
```python
import functools
import itertools

import jax
import jax.numpy as jnp
from jax import lax
from jax.experimental import pallas as pl
from jax.experimental.pallas import tpu as pltpu
from jax.sharding import PartitionSpec as P

GAMMA = 1.4
EPS = 1e-06 * (3.0 / 16.0)
COURANT = 0.4
MESH = pl.DeviceIdType.MESH
AXES = ("gx", "gy", "gz")
ORDERS = ([0, 1, 2, 3, 4], [0, 2, 1, 3, 4], [0, 3, 1, 2, 4])
LANES = 128
FIELD = 12
STATE = 5 * FIELD
LINEAR = STATE + 6
KEPT = LINEAR + 10


def project(u, vn, va, vb, kin, b1h, ich):
    a = u[4] + kin * u[0] - vn * u[1] - va * u[2] - vb * u[3]
    a = b1h * a
    b = (vn * u[0] - u[1]) * ich
    return [a + b, u[2] - va * u[0], u[3] - vb * u[0], u[0] - (a + a), a - b]


def nonlinear(e1, e2, e3, h):
    c = ((4.0 / 3.0) * h) * h + EPS
    g = h + 0.75 * e2
    q0 = 1.0 / (e1 * (e1 + h) + c)
    q1 = 1.0 / (e2 * (e2 + h) + c)
    q2 = 1.0 / (e3 * (e3 - g) + (((4.0 / 3.0) * g) * g + EPS))
    w0 = q0 * q0
    w2 = 3.0 * (q2 * q2)
    n0 = e1 - e2
    return (w0 * (n0 + n0) + w2 * (e2 - e3)) / (w0 + w2 + 6.0 * (q1 * q1))


def rows_of(j):
    return pl.ds(pl.multiple_of(8 * j, 8), 8)


class Sweep:
    def __init__(self, direction, slots, lane_rows, q, work, kept):
        self.order = ORDERS[direction]
        self.slots, self.r = slots, lane_rows
        self.q, self.work, self.kept = q, work, kept

    def cell(self, j):
        s = [self.q[c, rows_of(j), :] for c in self.order]
        inv = 1.0 / s[0]
        vq = s[1] * (0.25 * inv)
        pq = 0.25 * (GAMMA - 1.0) * (s[4] - (0.5 * inv) * (s[1] * s[1] + s[2] * s[2] + s[3] * s[3]))
        f = [0.25 * s[1], s[1] * vq + pq, s[2] * vq, s[3] * vq, s[4] * vq + 4.0 * (pq * vq)]
        for c in range(5):
            self.work[j, c] = f[c]

    def differ(self, j):
        r = self.r
        for c in range(5):
            flux = [self.work[j + k * r, c] for k in (-1, 0, 1)]
            state = [self.q[self.order[c], rows_of(j + k * r), :] for k in (-1, 0, 1)]
            for place, (low, mid, high) in ((5, flux), (10, state)):
                below = mid - low
                self.work[j, place + c] = (high - mid) - below
                self.work[j, place + 10 + c] = 0.75 * below

    def face(self, j):
        q, work, kept, r = self.q, self.work, self.kept, self.r
        mean = [q[c, rows_of(j + 2 * r), :] + q[c, rows_of(j + 3 * r), :] for c in self.order]
        inv = 1.0 / mean[0]
        vn, va, vb = mean[1] * inv, mean[2] * inv, mean[3] * inv
        kin = 0.5 * (vn * vn + va * va + vb * vb)
        c2 = GAMMA * (GAMMA - 1.0) * (mean[4] * inv - kin)
        ic = lax.rsqrt(c2)
        args = (vn, va, vb, kin, (0.5 * (GAMMA - 1.0)) * (ic * ic), 0.5 * ic)
        state = (vn, va, vb, kin, c2 * ic, (1.0 / (GAMMA - 1.0)) * c2 + kin)
        for k in range(6):
            kept[j, STATE + k] = state[k]
        places = [(k, 5, k - 1) for k in (1, 2, 3, 4)] + [(k, 10, k + 3) for k in (1, 2, 3, 4)]
        places += [(2, 15, 8), (4, 15, 9), (2, 20, 10), (4, 20, 11)]
        for cell, place, slot in places:
            u = project([work[j + cell * r, place + c] for c in range(5)], *args)
            for k in range(5):
                kept[j, FIELD * k + slot] = u[k]
        for c in range(5):
            near, far = work[j + 2 * r, c], work[j + 3 * r, c]
            kept[j, LINEAR + c] = 6.0 * (near + far) - work[j + 2 * r, 5 + c] - work[j + 3 * r, 5 + c]
            kept[j, LINEAR + 5 + c] = work[j + 3 * r, 10 + c] - work[j + 2 * r, 10 + c]

    def run(self, step, low, high, unroll=1):
        def body(t, _):
            step(t + low * self.r)
            return 0

        lax.fori_loop(0, (high - low) * self.r, body, 0, unroll=unroll)

    def run_two(self, step, low, high, width, unroll=1):
        def body(t, _):
            step(t + low * self.r + (t // (width * self.r)) * ((high - low - width) * self.r))
            return 0

        lax.fori_loop(0, 2 * width * self.r, body, 0, unroll=unroll)

    def inside(self):
        n = self.slots
        self.run(self.cell, 3, n + 3, 2)
        self.run(self.differ, 4, n + 2, 2)
        self.run(self.face, 3, n - 2)

    def outside(self):
        n = self.slots
        self.run_two(self.cell, 0, n + 3, 3, 2)
        self.run_two(self.differ, 1, n + 2, 3, 2)
        self.run_two(self.face, 0, n - 2, 3)


def face_flux(order, quarter, kept, j):
    n = []
    for k in range(5):
        a1, a2, a3, a4, b1, b2, b3, b4, ha, hb, sa, sb = (kept[j, FIELD * k + i] for i in range(FIELD))
        t2, t3 = quarter * b2, quarter * b3
        left = nonlinear(a1 + quarter * b1, a2 + t2, a3 + t3, ha + quarter * sa)
        right = nonlinear(a4 - quarter * b4, a3 - t3, a2 - t2, quarter * sb - hb)
        n.append(left + right)
    vn, va, vb, kin, sound, enthalpy = (kept[j, STATE + i] for i in range(6))
    d = sound * (n[4] - n[0])
    s15 = n[0] + n[4]
    s = s15 + n[3]
    out = [
        s,
        vn * s + d,
        va * s + n[1],
        vb * s + n[2],
        enthalpy * s15 + vn * d + va * n[1] + vb * n[2] + kin * n[3],
    ]
    flux = [None] * 5
    for c in range(5):
        flux[order[c]] = (kept[j, LINEAR + c] + quarter * kept[j, LINEAR + 5 + c]) + out[c]
    return flux


def gather_kernel(
    sizes, stages, shape, cons_hbm, cons, kept_x, kept_y, kept_z, speeds, qx, qy, qz, wx, wy, wz,
    xh, yh, zh, ysend, zsend, mine, theirs, halo_send, halo_recv, max_send, max_recv, load_sem,
):
    lx, ly, lz = shape
    rows = lx * ly
    groups = rows // LANES
    blocks = 8 // groups
    inner = lz // blocks
    load = pltpu.make_async_copy(cons_hbm, cons, load_sem)
    load.start()
    here = [lax.axis_index(axis) for axis in AXES]
    peers = []
    for axes in stages:
        group = []
        for shift in itertools.product(*[range(sizes[a]) for a in axes]):
            if any(shift):
                group.append({AXES[a]: lax.rem(here[a] + k, sizes[a]) for a, k in zip(axes, shift)})
        peers.append(group)
    barrier = pltpu.get_barrier_semaphore()
    count = 0
    for group in peers:
        for peer in group:
            pl.semaphore_signal(barrier, inc=1, device_id=peer, device_id_type=MESH)
            count += 1
    load.wait()

    best = [None] * 3
    for j in range(rows // 8):
        q = [cons[c, pl.ds(8 * j, 8), :] for c in range(5)]
        inv = 1.0 / q[0]
        vel = [q[d] * inv for d in (1, 2, 3)]
        kinetic = 0.5 * (vel[0] * vel[0] + vel[1] * vel[1] + vel[2] * vel[2])
        sound = jnp.sqrt((GAMMA * (GAMMA - 1.0)) * (q[4] * inv - kinetic))
        for d in range(3):
            value = jnp.abs(vel[d]) + sound
            best[d] = value if best[d] is None else jnp.maximum(best[d], value)
    for d in range(3):
        mine[0, pl.ds(d, 1), :] = jnp.max(best[d], axis=0, keepdims=True)
    mine[0, pl.ds(3, 5), :] = jnp.zeros((5, LANES), jnp.float32)

    for c in range(5):
        for k in range(3):
            ysend[0, c, pl.ds(k * lx, lx), :] = cons[c, pl.ds(ly - 3 + k, lx, stride=ly), :]
            ysend[1, c, pl.ds(k * lx, lx), :] = cons[c, pl.ds(k, lx, stride=ly), :]
    for c in range(5):
        for g in range(groups):
            turned = jnp.transpose(cons[c, pl.ds(g * LANES, LANES), :])
            for b in range(blocks):
                qz[c, pl.ds(24 + b * groups + g, inner, stride=8), :] = turned[b * inner:(b + 1) * inner]
            for k in range(3):
                zsend[0, c, k, g:g + 1, :] = turned[lz - 3 + k:lz - 2 + k]
                zsend[1, c, k, g:g + 1, :] = turned[k:k + 1]
    x_edge, y_edge = 3 * ly, 3 * lx
    for c in range(5):
        for y in range(ly):
            qy[c, pl.ds(y_edge + y * lx, lx), :] = cons[c, pl.ds(y, lx, stride=ly), :]
    qx[:, pl.ds(x_edge, rows), :] = cons[...]

    along = [
        Sweep(0, lx, ly // 8, qx, wx, kept_x),
        Sweep(1, ly, lx // 8, qy, wy, kept_y),
        Sweep(2, inner, 1, qz, wz, kept_z),
    ]
    along[1].inside()

    def halo(slot, src, dst, axis, up):
        me, size = here[axis], sizes[axis]
        target = lax.rem(me + (1 if up else size - 1), size)
        return pltpu.make_async_remote_copy(
            src_ref=src, dst_ref=dst, send_sem=halo_send.at[slot], recv_sem=halo_recv.at[slot],
            device_id={AXES[axis]: target}, device_id_type=MESH,
        )

    def spread(stage):
        copies = []
        first = sum(len(group) for group in peers[:stage])
        for k, peer in enumerate(peers[stage]):
            slot = first + k
            copy = pltpu.make_async_remote_copy(
                src_ref=mine.at[stage], dst_ref=theirs.at[slot],
                send_sem=max_send.at[slot], recv_sem=max_recv.at[slot],
                device_id=peer, device_id_type=MESH,
            )
            copy.start()
            copies.append((slot, copy))
        return copies

    def gather(stage, copies):
        value = mine[stage]
        for slot, copy in copies:
            copy.wait_recv()
            value = jnp.maximum(value, theirs[slot])
        return value

    pl.semaphore_wait(barrier, count)
    sent = [spread(0)]
    halos = [
        [
            halo(0, cons.at[:, pl.ds(rows - x_edge, x_edge), :], xh.at[0], 0, True),
            halo(1, cons.at[:, pl.ds(0, x_edge), :], xh.at[1], 0, False),
        ],
        [halo(2, ysend.at[0], yh.at[0], 1, True), halo(3, ysend.at[1], yh.at[1], 1, False)],
        [halo(4, zsend.at[0], zh.at[0], 2, True), halo(5, zsend.at[1], zh.at[1], 2, False)],
    ]
    for axis in (2, 1, 0):
        for copy in halos[axis]:
            copy.start()

    def fill_y():
        for copy in halos[1]:
            copy.wait()
        qy[:, pl.ds(0, y_edge), :] = yh[0]
        qy[:, pl.ds(y_edge + rows, y_edge), :] = yh[1]
        along[1].outside()

    def fill_z():
        for copy in halos[2]:
            copy.wait()
        size = inner * 8
        for c in range(5):
            for k in range(3):
                low, high = 8 * k, 24 + size + 8 * k
                qz[c, low:low + groups, :] = zh[0, c, k]
                qz[c, low + groups:low + 8, :] = qz[c, size + 8 * k:size + 8 + 8 * k - groups, :]
                qz[c, high:high + 8 - groups, :] = qz[c, 24 + 8 * k + groups:32 + 8 * k, :]
                qz[c, high + 8 - groups:high + 8, :] = zh[1, c, k]
        along[2].outside()

    def fill_x():
        for copy in halos[0]:
            copy.wait()
        qx[:, pl.ds(0, x_edge), :] = xh[0]
        qx[:, pl.ds(x_edge + rows, x_edge), :] = xh[1]
        along[0].outside()

    work = [along[2].inside, along[0].inside]
    work.pop(0)()
    for stage in range(1, len(stages)):
        mine[stage] = gather(stage - 1, sent[-1])
        sent.append(spread(stage))
        if work:
            work.pop(0)()
    for rest in work:
        rest()
    fill_y()
    fill_z()
    top = gather(len(stages) - 1, sent[-1])
    for copies in sent:
        for _, copy in copies:
            copy.wait_send()
    for d in range(3):
        largest = jnp.max(top[d:d + 1], axis=1, keepdims=True)
        speeds[d] = jnp.broadcast_to(largest, (8, LANES))
    fill_x()


def combine_kernel(
    cells, shape, cons, kept_x, kept_y, kept_z, speeds, out_hbm, tend, acc, out, tz, faces, store_sem,
):
    lx, ly, lz = shape
    rows = lx * ly
    groups = rows // LANES
    blocks = 8 // groups
    inner = lz // blocks
    speed = [speeds[d] for d in range(3)]
    step = COURANT / (speed[0] * cells[0] + speed[1] * cells[1] + speed[2] * cells[2])
    quarter = [0.25 * speed[d] for d in range(3)]
    scale = [step * (cells[d] / 3.0) for d in range(3)]

    def sweep(direction, r, kept, flux, place, low, high):
        def body(j, _):
            new = face_flux(ORDERS[direction], quarter[direction], kept, j)
            old = [flux[j, c] for c in range(5)]
            for c in range(5):
                flux[j + r, c] = new[c]
            for c in range(5):
                place(j, c, scale[direction] * (old[c] - new[c]))
            return 0

        lax.fori_loop(low * r, high * r, body, 0)

    ry, rx = lx // 8, ly // 8

    def place_y(j, c, value):
        y = jnp.maximum(j // ry - 1, 0)
        tend[c, pl.ds(8 * ly * (j % ry) + y, 8, stride=ly), :] = value

    def place_z(j, c, value):
        tz[c, rows_of(jnp.maximum(j - 1, 0)), :] = value

    def place_x(j, c, value):
        x = jnp.maximum(j // rx - 1, 0)
        here = rows_of(x * rx + j % rx)
        out[c, here, :] = acc[c, here, :] + value

    sweep(1, ry, kept_y, faces, place_y, 0, ly + 1)
    sweep(2, 1, kept_z, faces, place_z, 0, inner + 1)
    for c in range(5):
        for g in range(groups):
            parts = [tz[c, pl.ds(b * groups + g, inner, stride=8), :] for b in range(blocks)]
            turned = jnp.transpose(jnp.concatenate(parts, axis=0))
            here = pl.ds(g * LANES, LANES)
            acc[c, here, :] = (cons[c, here, :] + tend[c, here, :]) + turned
    stores = []
    chunk = lx // 4
    for m in range(4):
        sweep(0, rx, kept_x, faces, place_x, 0 if m == 0 else m * chunk + 1, (m + 1) * chunk + 1)
        part = pl.ds(m * chunk * ly, chunk * ly)
        stores.append(pltpu.make_async_copy(out.at[:, part, :], out_hbm.at[:, part, :], store_sem.at[m]))
        stores[-1].start()
    for store in stores:
        store.wait()


def solution(mesh):
    sizes = [mesh.shape[axis] for axis in AXES]
    stages = [(0, 1), (2,)] if sizes[0] * sizes[1] <= 16 else [(0,), (2,), (1,)]

    def per_device(conserved):
        _, lx, ly, lz = conserved.shape
        shape = (lx, ly, lz)
        cells = [float(n * s) for n, s in zip(shape, sizes)]
        rows = lx * ly
        groups = rows // LANES
        inner = lz * groups // 8
        assert lz == LANES and rows % LANES == 0 and 8 % groups == 0 and lx % 8 == 0 and ly % 8 == 0
        total = 0
        for axes in stages:
            size = 1
            for a in axes:
                size *= sizes[a]
            total += size - 1

        def vmem(*dims):
            return pltpu.VMEM(dims, jnp.float32)

        def faces(count):
            return vmem(count, KEPT, 8, LANES)

        pads = [(lx + 6) * ly // 8, (ly + 6) * lx // 8, inner + 6]
        kept = [faces((lx + 1) * ly // 8), faces((ly + 1) * lx // 8), faces(inner + 1)]
        whole = pl.BlockSpec(memory_space=pltpu.VMEM)
        cons, kept_x, kept_y, kept_z, speeds = pl.pallas_call(
            functools.partial(gather_kernel, sizes, stages, shape),
            name="gather",
            out_shape=[vmem(5, rows, lz)] + kept + [vmem(3, 8, LANES)],
            in_specs=[pl.BlockSpec(memory_space=pltpu.HBM)],
            out_specs=[whole] * 5,
            scratch_shapes=[vmem(5, 8 * n, LANES) for n in pads] + [vmem(n, 25, 8, LANES) for n in pads] + [
                vmem(2, 5, 3 * ly, lz),
                vmem(2, 5, 3 * lx, lz),
                vmem(2, 5, 3, groups, LANES),
                vmem(2, 5, 3 * lx, lz),
                vmem(2, 5, 3, groups, LANES),
                vmem(len(stages), 8, LANES),
                vmem(total, 8, LANES),
                pltpu.SemaphoreType.DMA((6,)),
                pltpu.SemaphoreType.DMA((6,)),
                pltpu.SemaphoreType.DMA((total,)),
                pltpu.SemaphoreType.DMA((total,)),
                pltpu.SemaphoreType.DMA,
            ],
            compiler_params=pltpu.CompilerParams(
                collective_id=0, has_side_effects=True, vmem_limit_bytes=18 * 2**20
            ),
        )(pltpu.with_memory_space_constraint(conserved.reshape(5, rows, lz), pltpu.HBM))
        out = pl.pallas_call(
            functools.partial(combine_kernel, cells, shape),
            name="combine",
            out_shape=jax.ShapeDtypeStruct((5, rows, lz), jnp.float32),
            in_specs=[whole] * 5,
            out_specs=pl.BlockSpec(memory_space=pl.ANY),
            scratch_shapes=[vmem(5, rows, lz)] * 3 + [
                vmem(5, 8 * inner, LANES),
                vmem(max((lx + 2) * ly // 8, (ly + 2) * lx // 8, inner + 2), 5, 8, LANES),
                pltpu.SemaphoreType.DMA((4,)),
            ],
            compiler_params=pltpu.CompilerParams(vmem_limit_bytes=16 * 2**20),
        )(cons, kept_x, kept_y, kept_z, speeds)
        return out.reshape(conserved.shape)

    return jax.shard_map(
        per_device,
        mesh=mesh,
        in_specs=(P(None, "gx", "gy", "gz"),),
        out_specs=P(None, "gx", "gy", "gz"),
        check_vma=False,
    )
```

time: 30 us -> 24.9 us (0.83)
  Pallas kernels: 27.8 us -> 24.7 us
  local copies, waits for them, and re-layouts: 1.99 us -> 0 us
    pallas_call x1 -> x2, Pallas kernels: 27.8 us -> 24.7 us  [the longest x1 15.5 us: per_device(): pl.pallas_call(functools.partial(gather_kernel, sizes, stages, shape), na...]
    unnamed x1 -> x0, local copies, waits for them, and re-layouts: 1.99 us -> none
where the time goes in v1:
time: 24.9 us; the launch traced here: 24.7 us
  Pallas kernels  24.7 us (99%)
    pallas_call x1, Pallas kernels, per_device(): pl.pallas_call(functools.partial(gather_kernel, sizes, stages, shape), na...  15.5 us
    pallas_call x1, Pallas kernels, per_device(): pl.pallas_call(functools.partial(combine_kernel, cells, shape), name='com...  9.19 us

profile of v1, /device:TPU:0, one launch (start us, length us, event | category | flops | bytes accessed | tf_op | source)
XLA Modules:
  0.0 24.7 jit_solution(2960224016151681169)
XLA Ops:
  0.0 15.5 %gather.1 = (f32[5,256,128]{2,1,0:T(8,128)S(1)}, f32[34,76,8,128]{3,2,1,0:T(8,128)S(1)}, f32[34,76,8,128]{3,2,1,0:T(8,128)S(1)}, f32[33,76,8,128]{3,2,1,0:T(8,128)S(1)}, f32[3,8,128]{2,1,0:T(8,128)S(1)}) custom-call(f32[5,256,128]{2,1,0:T(8,128)} %bitcast.2), custom_call_target="tpu_custom_call" | custom-call | tf_op jit(solution)/shard_map/gather/pallas_call | solution.py:390
  15.6 9.2 %combine.1 = f32[5,256,128]{2,1,0:T(8,128)} custom-call(f32[5,256,128]{2,1,0:T(8,128)S(1)} %get-tuple-element.10.cons, f32[34,76,8,128]{3,2,1,0:T(8,128)S(1)} %get-tuple-element.11.kept_x, f32[34,76,8,128]{3,2,1,0:T(8,128)S(1)} %get-tuple-element.12.kept_y, f32[33,76,8,128]{3,2,1,0:T(8,128)S(1)} %get-tuple-element.13.kept_z, ...), custom_call_target="tpu_custom_call" | custom-call | tf_op jit(solution)/shard_map/combine/pallas_call | solution.py:414

commit v2 on v1

--- a/solution.py
+++ b/solution.py
@@ -99,24 +99,18 @@
 
         lax.fori_loop(0, (high - low) * self.r, body, 0, unroll=unroll)
 
-    def run_two(self, step, low, high, width, unroll=1):
-        def body(t, _):
-            step(t + low * self.r + (t // (width * self.r)) * ((high - low - width) * self.r))
-            return 0
-
-        lax.fori_loop(0, 2 * width * self.r, body, 0, unroll=unroll)
-
     def inside(self):
         n = self.slots
         self.run(self.cell, 3, n + 3, 2)
         self.run(self.differ, 4, n + 2, 2)
-        self.run(self.face, 3, n - 2)
+        self.run(self.face, 3, n - 2, 2)
 
     def outside(self):
         n = self.slots
-        self.run_two(self.cell, 0, n + 3, 3, 2)
-        self.run_two(self.differ, 1, n + 2, 3, 2)
-        self.run_two(self.face, 0, n - 2, 3)
+        for first, step, unroll in ((0, self.cell, 3), (1, self.differ, 3), (0, self.face, 3)):
+            shift = n + 3 - 2 * first if step != self.face else n - 2
+            self.run(step, first, first + 3, unroll)
+            self.run(step, first + shift, first + shift + 3, unroll)
 
 
 def face_flux(order, quarter, kept, j):
@@ -144,8 +138,21 @@
     return flux
 
 
+def sweep(direction, r, quarter, scale, kept, faces, place, low, high, unroll):
+    def body(j, _):
+        new = face_flux(ORDERS[direction], quarter, kept, j)
+        old = [faces[j, c] for c in range(5)]
+        for c in range(5):
+            faces[j + r, c] = new[c]
+        for c in range(5):
+            place(j, c, scale * (old[c] - new[c]))
+        return 0
+
+    lax.fori_loop(low * r, high * r, body, 0, unroll=unroll)
+
+
 def gather_kernel(
-    sizes, stages, shape, cons_hbm, cons, kept_x, kept_y, kept_z, speeds, qx, qy, qz, wx, wy, wz,
+    sizes, stages, cells, shape, cons_hbm, kept_x, acc, factors, cons, kept_y, kept_z, faces, tz, qx, qy, qz, wx, wy, wz,
     xh, yh, zh, ysend, zsend, mine, theirs, halo_send, halo_recv, max_send, max_recv, load_sem,
 ):
     lx, ly, lz = shape
@@ -155,13 +162,13 @@
     inner = lz // blocks
     load = pltpu.make_async_copy(cons_hbm, cons, load_sem)
     load.start()
-    here = [lax.axis_index(axis) for axis in AXES]
+    me = [lax.axis_index(axis) for axis in AXES]
     peers = []
     for axes in stages:
         group = []
         for shift in itertools.product(*[range(sizes[a]) for a in axes]):
             if any(shift):
-                group.append({AXES[a]: lax.rem(here[a] + k, sizes[a]) for a, k in zip(axes, shift)})
+                group.append({AXES[a]: lax.rem(me[a] + k, sizes[a]) for a, k in zip(axes, shift)})
         peers.append(group)
     barrier = pltpu.get_barrier_semaphore()
     count = 0
@@ -181,9 +188,9 @@
         for d in range(3):
             value = jnp.abs(vel[d]) + sound
             best[d] = value if best[d] is None else jnp.maximum(best[d], value)
-    for d in range(3):
-        mine[0, pl.ds(d, 1), :] = jnp.max(best[d], axis=0, keepdims=True)
-    mine[0, pl.ds(3, 5), :] = jnp.zeros((5, LANES), jnp.float32)
+    lane = lax.broadcasted_iota(jnp.int32, (1, LANES), 1)
+    local = [jnp.max(jnp.max(v, axis=0, keepdims=True), axis=1, keepdims=True) for v in best]
+    mine[0] = jnp.where(lane == 0, local[0], jnp.where(lane == 1, local[1], local[2]))
 
     for c in range(5):
         for k in range(3):
@@ -195,8 +202,8 @@
             for b in range(blocks):
                 qz[c, pl.ds(24 + b * groups + g, inner, stride=8), :] = turned[b * inner:(b + 1) * inner]
             for k in range(3):
-                zsend[0, c, k, g:g + 1, :] = turned[lz - 3 + k:lz - 2 + k]
-                zsend[1, c, k, g:g + 1, :] = turned[k:k + 1]
+                zsend[0, pl.ds((3 * c + k) * groups + g, 1), :] = turned[lz - 3 + k:lz - 2 + k]
+                zsend[1, pl.ds((3 * c + k) * groups + g, 1), :] = turned[k:k + 1]
     x_edge, y_edge = 3 * ly, 3 * lx
     for c in range(5):
         for y in range(ly):
@@ -208,11 +215,12 @@
         Sweep(1, ly, lx // 8, qy, wy, kept_y),
         Sweep(2, inner, 1, qz, wz, kept_z),
     ]
-    along[1].inside()
+    for axis in (0,):
+        along[axis].inside()
 
     def halo(slot, src, dst, axis, up):
-        me, size = here[axis], sizes[axis]
-        target = lax.rem(me + (1 if up else size - 1), size)
+        size = sizes[axis]
+        target = lax.rem(me[axis] + (1 if up else size - 1), size)
         return pltpu.make_async_remote_copy(
             src_ref=src, dst_ref=dst, send_sem=halo_send.at[slot], recv_sem=halo_recv.at[slot],
             device_id={AXES[axis]: target}, device_id_type=MESH,
@@ -267,10 +275,10 @@
         for c in range(5):
             for k in range(3):
                 low, high = 8 * k, 24 + size + 8 * k
-                qz[c, low:low + groups, :] = zh[0, c, k]
+                qz[c, low:low + groups, :] = zh[0, pl.ds((3 * c + k) * groups, groups), :]
                 qz[c, low + groups:low + 8, :] = qz[c, size + 8 * k:size + 8 + 8 * k - groups, :]
                 qz[c, high:high + 8 - groups, :] = qz[c, 24 + 8 * k + groups:32 + 8 * k, :]
-                qz[c, high + 8 - groups:high + 8, :] = zh[1, c, k]
+                qz[c, high + 8 - groups:high + 8, :] = zh[1, pl.ds((3 * c + k) * groups, groups), :]
         along[2].outside()
 
     def fill_x():
@@ -280,78 +288,57 @@
         qx[:, pl.ds(x_edge + rows, x_edge), :] = xh[1]
         along[0].outside()
 
-    work = [along[2].inside, along[0].inside]
-    work.pop(0)()
+    for axis in (2, 1):
+        along[axis].inside()
+    fill_y()
+    fill_z()
     for stage in range(1, len(stages)):
         mine[stage] = gather(stage - 1, sent[-1])
         sent.append(spread(stage))
-        if work:
-            work.pop(0)()
-    for rest in work:
-        rest()
-    fill_y()
-    fill_z()
     top = gather(len(stages) - 1, sent[-1])
     for copies in sent:
         for _, copy in copies:
             copy.wait_send()
-    for d in range(3):
-        largest = jnp.max(top[d:d + 1], axis=1, keepdims=True)
-        speeds[d] = jnp.broadcast_to(largest, (8, LANES))
-    fill_x()
-
-
-def combine_kernel(
-    cells, shape, cons, kept_x, kept_y, kept_z, speeds, out_hbm, tend, acc, out, tz, faces, store_sem,
-):
-    lx, ly, lz = shape
-    rows = lx * ly
-    groups = rows // LANES
-    blocks = 8 // groups
-    inner = lz // blocks
-    speed = [speeds[d] for d in range(3)]
+    speed = [jnp.broadcast_to(top[:, d:d + 1], (8, LANES)) for d in range(3)]
     step = COURANT / (speed[0] * cells[0] + speed[1] * cells[1] + speed[2] * cells[2])
-    quarter = [0.25 * speed[d] for d in range(3)]
-    scale = [step * (cells[d] / 3.0) for d in range(3)]
-
-    def sweep(direction, r, kept, flux, place, low, high):
-        def body(j, _):
-            new = face_flux(ORDERS[direction], quarter[direction], kept, j)
-            old = [flux[j, c] for c in range(5)]
-            for c in range(5):
-                flux[j + r, c] = new[c]
-            for c in range(5):
-                place(j, c, scale[direction] * (old[c] - new[c]))
-            return 0
-
-        lax.fori_loop(low * r, high * r, body, 0)
-
-    ry, rx = lx // 8, ly // 8
+    factors[0] = 0.25 * speed[0]
+    factors[1] = step * (cells[0] / 3.0)
+
+    ry = lx // 8
 
     def place_y(j, c, value):
         y = jnp.maximum(j // ry - 1, 0)
-        tend[c, pl.ds(8 * ly * (j % ry) + y, 8, stride=ly), :] = value
+        acc[c, pl.ds(8 * ly * (j % ry) + y, 8, stride=ly), :] = value
 
     def place_z(j, c, value):
         tz[c, rows_of(jnp.maximum(j - 1, 0)), :] = value
 
-    def place_x(j, c, value):
-        x = jnp.maximum(j // rx - 1, 0)
-        here = rows_of(x * rx + j % rx)
-        out[c, here, :] = acc[c, here, :] + value
-
-    sweep(1, ry, kept_y, faces, place_y, 0, ly + 1)
-    sweep(2, 1, kept_z, faces, place_z, 0, inner + 1)
+    for axis, r, slots, place in ((1, ry, ly, place_y), (2, 1, inner, place_z)):
+        scale = step * (cells[axis] / 3.0)
+        sweep(axis, r, 0.25 * speed[axis], scale, along[axis].kept, faces, place, 0, slots + 1, (2, 3)[axis - 1])
     for c in range(5):
         for g in range(groups):
             parts = [tz[c, pl.ds(b * groups + g, inner, stride=8), :] for b in range(blocks)]
             turned = jnp.transpose(jnp.concatenate(parts, axis=0))
             here = pl.ds(g * LANES, LANES)
-            acc[c, here, :] = (cons[c, here, :] + tend[c, here, :]) + turned
+            acc[c, here, :] = (cons[c, here, :] + acc[c, here, :]) + turned
+    fill_x()
+
+
+def combine_kernel(shape, kept, acc, factors, out_hbm, out, faces, store_sem):
+    lx, ly, lz = shape
+    rx = ly // 8
+    quarter, scale = factors[0], factors[1]
+
+    def place(j, c, value):
+        x = jnp.maximum(j // rx - 1, 0)
+        here = rows_of(x * rx + j % rx)
+        out[c, here, :] = acc[c, here, :] + value
+
     stores = []
     chunk = lx // 4
     for m in range(4):
-        sweep(0, rx, kept_x, faces, place_x, 0 if m == 0 else m * chunk + 1, (m + 1) * chunk + 1)
+        sweep(0, rx, quarter, scale, kept, faces, place, 0 if m == 0 else m * chunk + 1, (m + 1) * chunk + 1, 2)
         part = pl.ds(m * chunk * ly, chunk * ly)
         stores.append(pltpu.make_async_copy(out.at[:, part, :], out_hbm.at[:, part, :], store_sem.at[m]))
         stores[-1].start()
@@ -361,7 +348,7 @@
 
 def solution(mesh):
     sizes = [mesh.shape[axis] for axis in AXES]
-    stages = [(0, 1), (2,)] if sizes[0] * sizes[1] <= 16 else [(0,), (2,), (1,)]
+    stages = [(0, 1, 2)] if sizes[0] * sizes[1] * sizes[2] <= 64 else [(0,), (2,), (1,)]
 
     def per_device(conserved):
         _, lx, ly, lz = conserved.shape
@@ -386,21 +373,24 @@
 
         pads = [(lx + 6) * ly // 8, (ly + 6) * lx // 8, inner + 6]
         kept = [faces((lx + 1) * ly // 8), faces((ly + 1) * lx // 8), faces(inner + 1)]
+        flux = vmem(max((lx + 2) * ly // 8, (ly + 2) * lx // 8, inner + 2), 5, 8, LANES)
+        block = vmem(5, rows, lz)
         whole = pl.BlockSpec(memory_space=pltpu.VMEM)
-        cons, kept_x, kept_y, kept_z, speeds = pl.pallas_call(
-            functools.partial(gather_kernel, sizes, stages, shape),
+        kept_x, acc, factors = pl.pallas_call(
+            functools.partial(gather_kernel, sizes, stages, cells, shape),
             name="gather",
-            out_shape=[vmem(5, rows, lz)] + kept + [vmem(3, 8, LANES)],
+            out_shape=[kept[0], block, vmem(2, 8, LANES)],
             in_specs=[pl.BlockSpec(memory_space=pltpu.HBM)],
-            out_specs=[whole] * 5,
-            scratch_shapes=[vmem(5, 8 * n, LANES) for n in pads] + [vmem(n, 25, 8, LANES) for n in pads] + [
+            out_specs=[whole] * 3,
+            scratch_shapes=[block, kept[1], kept[2], flux, vmem(5, 8 * inner, LANES)]
+            + [vmem(5, 8 * n, LANES) for n in pads] + [vmem(n, 25, 8, LANES) for n in pads] + [
                 vmem(2, 5, 3 * ly, lz),
                 vmem(2, 5, 3 * lx, lz),
-                vmem(2, 5, 3, groups, LANES),
+                vmem(2, 15 * groups, LANES),
                 vmem(2, 5, 3 * lx, lz),
-                vmem(2, 5, 3, groups, LANES),
-                vmem(len(stages), 8, LANES),
-                vmem(total, 8, LANES),
+                vmem(2, 15 * groups, LANES),
+                vmem(len(stages), 1, LANES),
+                vmem(total, 1, LANES),
                 pltpu.SemaphoreType.DMA((6,)),
                 pltpu.SemaphoreType.DMA((6,)),
                 pltpu.SemaphoreType.DMA((total,)),
@@ -408,22 +398,18 @@
                 pltpu.SemaphoreType.DMA,
             ],
             compiler_params=pltpu.CompilerParams(
-                collective_id=0, has_side_effects=True, vmem_limit_bytes=18 * 2**20
+                collective_id=0, has_side_effects=True, vmem_limit_bytes=44 * 2**20
             ),
         )(pltpu.with_memory_space_constraint(conserved.reshape(5, rows, lz), pltpu.HBM))
         out = pl.pallas_call(
-            functools.partial(combine_kernel, cells, shape),
+            functools.partial(combine_kernel, shape),
             name="combine",
             out_shape=jax.ShapeDtypeStruct((5, rows, lz), jnp.float32),
-            in_specs=[whole] * 5,
+            in_specs=[whole] * 3,
             out_specs=pl.BlockSpec(memory_space=pl.ANY),
-            scratch_shapes=[vmem(5, rows, lz)] * 3 + [
-                vmem(5, 8 * inner, LANES),
-                vmem(max((lx + 2) * ly // 8, (ly + 2) * lx // 8, inner + 2), 5, 8, LANES),
-                pltpu.SemaphoreType.DMA((4,)),
-            ],
+            scratch_shapes=[block, flux, pltpu.SemaphoreType.DMA((4,))],
             compiler_params=pltpu.CompilerParams(vmem_limit_bytes=16 * 2**20),
-        )(cons, kept_x, kept_y, kept_z, speeds)
+        )(kept_x, acc, factors)
         return out.reshape(conserved.shape)
 
     return jax.shard_map(

time: 24.9 us -> 21.8 us (0.88)
  Pallas kernels: 24.7 us -> 21.6 us
    pallas_call x2, Pallas kernels: 24.7 us -> 21.6 us  [the longest x1 18.4 us: per_device(): pl.pallas_call(functools.partial(gather_kernel, sizes, stages, cells, sha...]
where the time goes in v2:
time: 21.8 us; the launch traced here: 21.6 us
  Pallas kernels  21.6 us (99%)
    pallas_call x1, Pallas kernels, per_device(): pl.pallas_call(functools.partial(gather_kernel, sizes, stages, cells, sha...  18.4 us
    pallas_call x1, Pallas kernels, per_device(): pl.pallas_call(functools.partial(combine_kernel, shape), name='combine',...  3.17 us

profile of v2, /device:TPU:0, one launch (start us, length us, event | category | flops | bytes accessed | tf_op | source)
XLA Modules:
  0.0 21.6 jit_solution(425721440492620129)
XLA Ops:
  0.0 18.4 %gather.1 = (f32[34,76,8,128]{3,2,1,0:T(8,128)S(1)}, f32[5,256,128]{2,1,0:T(8,128)S(1)}, f32[2,8,128]{2,1,0:T(8,128)S(1)}) custom-call(f32[5,256,128]{2,1,0:T(8,128)} %bitcast.2), custom_call_target="tpu_custom_call" | custom-call | tf_op jit(solution)/shard_map/gather/pallas_call | solution.py:379
  18.4 3.2 %combine.1 = f32[5,256,128]{2,1,0:T(8,128)} custom-call(f32[34,76,8,128]{3,2,1,0:T(8,128)S(1)} %get-tuple-element.8.kept, f32[5,256,128]{2,1,0:T(8,128)S(1)} %get-tuple-element.9.acc, f32[2,8,128]{2,1,0:T(8,128)S(1)} %get-tuple-element.10.factors), custom_call_target="tpu_custom_call" | custom-call | tf_op jit(solution)/shard_map/combine/pallas_call | solution.py:404

commit v3 on v2

--- a/solution.py
+++ b/solution.py
@@ -1,5 +1,4 @@
 import functools
-import itertools
 
 import jax
 import jax.numpy as jnp
@@ -99,11 +98,17 @@
 
         lax.fori_loop(0, (high - low) * self.r, body, 0, unroll=unroll)
 
+    def cells_inside(self):
+        n = self.slots
+        self.run(self.cell, 3, n + 3, 4)
+        self.run(self.differ, 4, n + 2, 4 if self.r > 1 else 6)
+
+    def faces_inside(self):
+        self.run(self.face, 3, self.slots - 2, 4 - self.r)
+
     def inside(self):
-        n = self.slots
-        self.run(self.cell, 3, n + 3, 2)
-        self.run(self.differ, 4, n + 2, 2)
-        self.run(self.face, 3, n - 2, 2)
+        self.cells_inside()
+        self.faces_inside()
 
     def outside(self):
         n = self.slots
@@ -145,42 +150,63 @@
         for c in range(5):
             faces[j + r, c] = new[c]
         for c in range(5):
-            place(j, c, scale * (old[c] - new[c]))
+            change = old[c] - new[c]
+            place(j, c, change if scale is None else scale * change)
         return 0
 
     lax.fori_loop(low * r, high * r, body, 0, unroll=unroll)
 
 
 def gather_kernel(
-    sizes, stages, cells, shape, cons_hbm, kept_x, acc, factors, cons, kept_y, kept_z, faces, tz, qx, qy, qz, wx, wy, wz,
-    xh, yh, zh, ysend, zsend, mine, theirs, halo_send, halo_recv, max_send, max_recv, load_sem,
+    sizes, cells, shape, cons_hbm, kept_x, acc, factors, kept_y, kept_z, faces, tz, qx, qy, qz, wx, wy, wz,
+    zh, zsend, top, mine, theirs, halo_send, halo_recv, max_send, max_recv, load_sem, turn_sem,
 ):
     lx, ly, lz = shape
     rows = lx * ly
     groups = rows // LANES
     blocks = 8 // groups
     inner = lz // blocks
-    load = pltpu.make_async_copy(cons_hbm, cons, load_sem)
+    x_edge, y_edge = 3 * ly, 3 * lx
+    cons = qx.at[:, pl.ds(x_edge, rows), :]
+    turned_y = qy.at[:, pl.ds(y_edge, rows), :]
+    load = pltpu.make_async_copy(cons_hbm.reshape(5, rows, lz), cons, load_sem)
     load.start()
+    for y in range(ly):
+        pltpu.make_async_copy(cons_hbm.at[:, :, y, :], qy.at[:, pl.ds(y_edge + y * lx, lx), :], turn_sem).start()
     me = [lax.axis_index(axis) for axis in AXES]
-    peers = []
-    for axes in stages:
-        group = []
-        for shift in itertools.product(*[range(sizes[a]) for a in axes]):
-            if any(shift):
-                group.append({AXES[a]: lax.rem(me[a] + k, sizes[a]) for a, k in zip(axes, shift)})
-        peers.append(group)
+    count = sizes[0] * sizes[1] * sizes[2]
+    plane = sizes[0] * sizes[2]
+    place = (me[0] * sizes[1] + me[1]) * sizes[2] + me[2]
+    is_root = me[0] + me[2] == 0
+    roots = [{"gx": 0, "gy": r, "gz": 0} for r in range(sizes[1])]
+
+    def beside(axis, up):
+        return {AXES[axis]: lax.rem(me[axis] + (1 if up else sizes[axis] - 1), sizes[axis])}
+
     barrier = pltpu.get_barrier_semaphore()
-    count = 0
-    for group in peers:
-        for peer in group:
-            pl.semaphore_signal(barrier, inc=1, device_id=peer, device_id_type=MESH)
-            count += 1
+
+    def greet(peer):
+        pl.semaphore_signal(barrier, inc=1, device_id=peer, device_id_type=MESH)
+
+    for axis in range(3):
+        for up in (True, False):
+            greet(beside(axis, up))
+
+    @pl.when(is_root)
+    def _():
+        def tell(t, _):
+            other = lax.rem(place + t, count)
+            rest = other // sizes[2]
+            greet({"gx": rest // sizes[1], "gy": rest % sizes[1], "gz": other % sizes[2]})
+            return 0
+
+        lax.fori_loop(1, count, tell, 0)
+
     load.wait()
 
     best = [None] * 3
     for j in range(rows // 8):
-        q = [cons[c, pl.ds(8 * j, 8), :] for c in range(5)]
+        q = [qx[c, pl.ds(x_edge + 8 * j, 8), :] for c in range(5)]
         inv = 1.0 / q[0]
         vel = [q[d] * inv for d in (1, 2, 3)]
         kinetic = 0.5 * (vel[0] * vel[0] + vel[1] * vel[1] + vel[2] * vel[2])
@@ -190,71 +216,53 @@
             best[d] = value if best[d] is None else jnp.maximum(best[d], value)
     lane = lax.broadcasted_iota(jnp.int32, (1, LANES), 1)
     local = [jnp.max(jnp.max(v, axis=0, keepdims=True), axis=1, keepdims=True) for v in best]
-    mine[0] = jnp.where(lane == 0, local[0], jnp.where(lane == 1, local[1], local[2]))
-
-    for c in range(5):
-        for k in range(3):
-            ysend[0, c, pl.ds(k * lx, lx), :] = cons[c, pl.ds(ly - 3 + k, lx, stride=ly), :]
-            ysend[1, c, pl.ds(k * lx, lx), :] = cons[c, pl.ds(k, lx, stride=ly), :]
+    mine[...] = jnp.where(lane == 0, local[0], jnp.where(lane == 1, local[1], local[2]))
+
     for c in range(5):
         for g in range(groups):
-            turned = jnp.transpose(cons[c, pl.ds(g * LANES, LANES), :])
+            turned = jnp.transpose(qx[c, pl.ds(x_edge + g * LANES, LANES), :])
             for b in range(blocks):
                 qz[c, pl.ds(24 + b * groups + g, inner, stride=8), :] = turned[b * inner:(b + 1) * inner]
             for k in range(3):
                 zsend[0, pl.ds((3 * c + k) * groups + g, 1), :] = turned[lz - 3 + k:lz - 2 + k]
                 zsend[1, pl.ds((3 * c + k) * groups + g, 1), :] = turned[k:k + 1]
-    x_edge, y_edge = 3 * ly, 3 * lx
-    for c in range(5):
-        for y in range(ly):
-            qy[c, pl.ds(y_edge + y * lx, lx), :] = cons[c, pl.ds(y, lx, stride=ly), :]
-    qx[:, pl.ds(x_edge, rows), :] = cons[...]
-
     along = [
         Sweep(0, lx, ly // 8, qx, wx, kept_x),
         Sweep(1, ly, lx // 8, qy, wy, kept_y),
         Sweep(2, inner, 1, qz, wz, kept_z),
     ]
-    for axis in (0,):
-        along[axis].inside()
+    pltpu.make_async_copy(turned_y, turned_y, turn_sem).wait()
+
+    @pl.when(is_root)
+    def _():
+        for axis in (0,):
+            along[axis].inside()
 
     def halo(slot, src, dst, axis, up):
-        size = sizes[axis]
-        target = lax.rem(me[axis] + (1 if up else size - 1), size)
         return pltpu.make_async_remote_copy(
             src_ref=src, dst_ref=dst, send_sem=halo_send.at[slot], recv_sem=halo_recv.at[slot],
-            device_id={AXES[axis]: target}, device_id_type=MESH,
+            device_id=beside(axis, up), device_id_type=MESH,
         )
 
-    def spread(stage):
-        copies = []
-        first = sum(len(group) for group in peers[:stage])
-        for k, peer in enumerate(peers[stage]):
-            slot = first + k
-            copy = pltpu.make_async_remote_copy(
-                src_ref=mine.at[stage], dst_ref=theirs.at[slot],
-                send_sem=max_send.at[slot], recv_sem=max_recv.at[slot],
-                device_id=peer, device_id_type=MESH,
-            )
-            copy.start()
-            copies.append((slot, copy))
-        return copies
-
-    def gather(stage, copies):
-        value = mine[stage]
-        for slot, copy in copies:
-            copy.wait_recv()
-            value = jnp.maximum(value, theirs[slot])
-        return value
-
-    pl.semaphore_wait(barrier, count)
-    sent = [spread(0)]
+    pl.semaphore_wait(barrier, 6 + sizes[1] - jnp.where(is_root, 1, 0))
+    reports = []
+    for r, root in enumerate(roots):
+        slot = lax.rem(place - r * sizes[2] + count - 1, count)
+        report = pltpu.make_async_remote_copy(
+            src_ref=mine, dst_ref=theirs.at[slot], send_sem=max_send.at[r], recv_sem=max_recv.at[0],
+            device_id=root, device_id_type=MESH,
+        )
+        pl.when(place != r * sizes[2])(report.start)
+        reports.append(report)
     halos = [
         [
-            halo(0, cons.at[:, pl.ds(rows - x_edge, x_edge), :], xh.at[0], 0, True),
-            halo(1, cons.at[:, pl.ds(0, x_edge), :], xh.at[1], 0, False),
+            halo(0, qx.at[:, pl.ds(rows, x_edge), :], qx.at[:, pl.ds(0, x_edge), :], 0, True),
+            halo(1, qx.at[:, pl.ds(x_edge, x_edge), :], qx.at[:, pl.ds(x_edge + rows, x_edge), :], 0, False),
         ],
-        [halo(2, ysend.at[0], yh.at[0], 1, True), halo(3, ysend.at[1], yh.at[1], 1, False)],
+        [
+            halo(2, qy.at[:, pl.ds(rows, y_edge), :], qy.at[:, pl.ds(0, y_edge), :], 1, True),
+            halo(3, qy.at[:, pl.ds(y_edge, y_edge), :], qy.at[:, pl.ds(y_edge + rows, y_edge), :], 1, False),
+        ],
         [halo(4, zsend.at[0], zh.at[0], 2, True), halo(5, zsend.at[1], zh.at[1], 2, False)],
     ]
     for axis in (2, 1, 0):
@@ -264,8 +272,6 @@
     def fill_y():
         for copy in halos[1]:
             copy.wait()
-        qy[:, pl.ds(0, y_edge), :] = yh[0]
-        qy[:, pl.ds(y_edge + rows, y_edge), :] = yh[1]
         along[1].outside()
 
     def fill_z():
@@ -284,22 +290,45 @@
     def fill_x():
         for copy in halos[0]:
             copy.wait()
-        qx[:, pl.ds(0, x_edge), :] = xh[0]
-        qx[:, pl.ds(x_edge + rows, x_edge), :] = xh[1]
         along[0].outside()
 
-    for axis in (2, 1):
-        along[axis].inside()
-    fill_y()
-    fill_z()
-    for stage in range(1, len(stages)):
-        mine[stage] = gather(stage - 1, sent[-1])
-        sent.append(spread(stage))
-    top = gather(len(stages) - 1, sent[-1])
-    for copies in sent:
-        for _, copy in copies:
-            copy.wait_send()
-    speed = [jnp.broadcast_to(top[:, d:d + 1], (8, LANES)) for d in range(3)]
+    def answer(peer):
+        return pltpu.make_async_remote_copy(
+            src_ref=top, dst_ref=top, send_sem=max_send.at[sizes[1]], recv_sem=max_recv.at[1],
+            device_id=peer, device_id_type=MESH,
+        )
+
+    def bytes_of(refs, send, receive):
+        return pltpu.make_async_remote_copy(
+            src_ref=refs, dst_ref=refs, send_sem=max_send.at[send], recv_sem=max_recv.at[receive],
+            device_id=beside(1, True), device_id_type=MESH,
+        )
+
+    @pl.when(is_root)
+    def _():
+        for axis in (2, 1):
+            along[axis].inside()
+        fill_y()
+        bytes_of(theirs, 0, 0).wait_recv()
+        top[...] = jnp.maximum(mine[...], jnp.max(theirs[...], axis=0))
+
+        def tell(t, _):
+            answer({"gx": t // sizes[2], "gy": me[1], "gz": t % sizes[2]}).start()
+            return 0
+
+        lax.fori_loop(1, plane, tell, 0)
+
+    @pl.when(jnp.logical_not(is_root))
+    def _():
+        for axis in (1, 2, 0):
+            along[axis].inside()
+        fill_y()
+        fill_z()
+        answer(beside(1, True)).wait_recv()
+
+    for r, report in enumerate(reports):
+        pl.when(place != r * sizes[2])(report.wait_send)
+    speed = [jnp.broadcast_to(top[0:1, d:d + 1], (8, LANES)) for d in range(3)]
     step = COURANT / (speed[0] * cells[0] + speed[1] * cells[1] + speed[2] * cells[2])
     factors[0] = 0.25 * speed[0]
     factors[1] = step * (cells[0] / 3.0)
@@ -313,16 +342,25 @@
     def place_z(j, c, value):
         tz[c, rows_of(jnp.maximum(j - 1, 0)), :] = value
 
-    for axis, r, slots, place in ((1, ry, ly, place_y), (2, 1, inner, place_z)):
-        scale = step * (cells[axis] / 3.0)
-        sweep(axis, r, 0.25 * speed[axis], scale, along[axis].kept, faces, place, 0, slots + 1, (2, 3)[axis - 1])
+    def combine(axis, r, slots, put, unroll):
+        sweep(axis, r, 0.25 * speed[axis], None, along[axis].kept, faces, put, 0, slots + 1, unroll)
+
+    combine(1, ry, ly, place_y, 2)
+    pl.when(is_root)(fill_z)
+    combine(2, 1, inner, place_z, 3)
+    scale = [(step * (cells[d] / 3.0))[:1] for d in range(3)]
     for c in range(5):
         for g in range(groups):
             parts = [tz[c, pl.ds(b * groups + g, inner, stride=8), :] for b in range(blocks)]
             turned = jnp.transpose(jnp.concatenate(parts, axis=0))
             here = pl.ds(g * LANES, LANES)
-            acc[c, here, :] = (cons[c, here, :] + acc[c, here, :]) + turned
+            held = qx[c, pl.ds(x_edge + g * LANES, LANES), :] + scale[1] * acc[c, here, :]
+            acc[c, here, :] = held + scale[2] * turned
     fill_x()
+
+    @pl.when(is_root)
+    def _():
+        bytes_of(theirs.at[pl.ds(0, plane - 1)], sizes[1], 1).wait_send()
 
 
 def combine_kernel(shape, kept, acc, factors, out_hbm, out, faces, store_sem):
@@ -348,7 +386,7 @@
 
 def solution(mesh):
     sizes = [mesh.shape[axis] for axis in AXES]
-    stages = [(0, 1, 2)] if sizes[0] * sizes[1] * sizes[2] <= 64 else [(0,), (2,), (1,)]
+    count = sizes[0] * sizes[1] * sizes[2]
 
     def per_device(conserved):
         _, lx, ly, lz = conserved.shape
@@ -358,13 +396,6 @@
         groups = rows // LANES
         inner = lz * groups // 8
         assert lz == LANES and rows % LANES == 0 and 8 % groups == 0 and lx % 8 == 0 and ly % 8 == 0
-        total = 0
-        for axes in stages:
-            size = 1
-            for a in axes:
-                size *= sizes[a]
-            total += size - 1
-
         def vmem(*dims):
             return pltpu.VMEM(dims, jnp.float32)
 
@@ -377,30 +408,29 @@
         block = vmem(5, rows, lz)
         whole = pl.BlockSpec(memory_space=pltpu.VMEM)
         kept_x, acc, factors = pl.pallas_call(
-            functools.partial(gather_kernel, sizes, stages, cells, shape),
+            functools.partial(gather_kernel, sizes, cells, shape),
             name="gather",
             out_shape=[kept[0], block, vmem(2, 8, LANES)],
             in_specs=[pl.BlockSpec(memory_space=pltpu.HBM)],
             out_specs=[whole] * 3,
-            scratch_shapes=[block, kept[1], kept[2], flux, vmem(5, 8 * inner, LANES)]
+            scratch_shapes=[kept[1], kept[2], flux, vmem(5, 8 * inner, LANES)]
             + [vmem(5, 8 * n, LANES) for n in pads] + [vmem(n, 25, 8, LANES) for n in pads] + [
-                vmem(2, 5, 3 * ly, lz),
-                vmem(2, 5, 3 * lx, lz),
                 vmem(2, 15 * groups, LANES),
-                vmem(2, 5, 3 * lx, lz),
                 vmem(2, 15 * groups, LANES),
-                vmem(len(stages), 1, LANES),
-                vmem(total, 1, LANES),
+                vmem(1, LANES),
+                vmem(1, LANES),
+                vmem(count - 1, 1, LANES),
                 pltpu.SemaphoreType.DMA((6,)),
                 pltpu.SemaphoreType.DMA((6,)),
-                pltpu.SemaphoreType.DMA((total,)),
-                pltpu.SemaphoreType.DMA((total,)),
+                pltpu.SemaphoreType.DMA((sizes[1] + 1,)),
+                pltpu.SemaphoreType.DMA((2,)),
+                pltpu.SemaphoreType.DMA,
                 pltpu.SemaphoreType.DMA,
             ],
             compiler_params=pltpu.CompilerParams(
                 collective_id=0, has_side_effects=True, vmem_limit_bytes=44 * 2**20
             ),
-        )(pltpu.with_memory_space_constraint(conserved.reshape(5, rows, lz), pltpu.HBM))
+        )(pltpu.with_memory_space_constraint(conserved, pltpu.HBM))
         out = pl.pallas_call(
             functools.partial(combine_kernel, shape),
             name="combine",

time: 21.8 us -> 20 us (0.917)
  Pallas kernels: 21.6 us -> 19.7 us
    pallas_call x1, Pallas kernels: 18.4 us -> 16.5 us  [per_device(): pl.pallas_call(functools.partial(gather_kernel, sizes, cells, shape), nam...]
where the time goes in v3:
time: 20 us; the launch traced here: 19.7 us
  Pallas kernels  19.7 us (98%)
    pallas_call x1, Pallas kernels, per_device(): pl.pallas_call(functools.partial(gather_kernel, sizes, cells, shape), nam...  16.5 us
    pallas_call x1, Pallas kernels, per_device(): pl.pallas_call(functools.partial(combine_kernel, shape), name='combine',...  3.17 us

profile of v3, /device:TPU:0, one launch (start us, length us, event | category | flops | bytes accessed | tf_op | source)
XLA Modules:
  0.0 19.7 jit_solution(4895462891599321401)
XLA Ops:
  0.0 16.5 %gather.1 = (f32[34,76,8,128]{3,2,1,0:T(8,128)S(1)}, f32[5,256,128]{2,1,0:T(8,128)S(1)}, f32[2,8,128]{2,1,0:T(8,128)S(1)}) custom-call(f32[5,16,16,128]{3,2,1,0:T(8,128)} %cons_hbm.1), custom_call_target="tpu_custom_call" | custom-call | tf_op jit(solution)/shard_map/gather/pallas_call | solution.py:410
  16.5 3.2 %combine.1 = f32[5,256,128]{2,1,0:T(8,128)} custom-call(f32[34,76,8,128]{3,2,1,0:T(8,128)S(1)} %get-tuple-element.8.kept, f32[5,256,128]{2,1,0:T(8,128)S(1)} %get-tuple-element.9.acc, f32[2,8,128]{2,1,0:T(8,128)S(1)} %get-tuple-element.10.factors), custom_call_target="tpu_custom_call" | custom-call | tf_op jit(solution)/shard_map/combine/pallas_call | solution.py:434

commit v4 on v3

--- a/solution.py
+++ b/solution.py
@@ -171,8 +171,6 @@
     turned_y = qy.at[:, pl.ds(y_edge, rows), :]
     load = pltpu.make_async_copy(cons_hbm.reshape(5, rows, lz), cons, load_sem)
     load.start()
-    for y in range(ly):
-        pltpu.make_async_copy(cons_hbm.at[:, :, y, :], qy.at[:, pl.ds(y_edge + y * lx, lx), :], turn_sem).start()
     me = [lax.axis_index(axis) for axis in AXES]
     count = sizes[0] * sizes[1] * sizes[2]
     plane = sizes[0] * sizes[2]
@@ -202,6 +200,8 @@
 
         lax.fori_loop(1, count, tell, 0)
 
+    for y in range(ly):
+        pltpu.make_async_copy(cons_hbm.at[:, :, y, :], qy.at[:, pl.ds(y_edge + y * lx, lx), :], turn_sem).start()
     load.wait()
 
     best = [None] * 3
@@ -218,21 +218,11 @@
     local = [jnp.max(jnp.max(v, axis=0, keepdims=True), axis=1, keepdims=True) for v in best]
     mine[...] = jnp.where(lane == 0, local[0], jnp.where(lane == 1, local[1], local[2]))
 
-    for c in range(5):
-        for g in range(groups):
-            turned = jnp.transpose(qx[c, pl.ds(x_edge + g * LANES, LANES), :])
-            for b in range(blocks):
-                qz[c, pl.ds(24 + b * groups + g, inner, stride=8), :] = turned[b * inner:(b + 1) * inner]
-            for k in range(3):
-                zsend[0, pl.ds((3 * c + k) * groups + g, 1), :] = turned[lz - 3 + k:lz - 2 + k]
-                zsend[1, pl.ds((3 * c + k) * groups + g, 1), :] = turned[k:k + 1]
     along = [
         Sweep(0, lx, ly // 8, qx, wx, kept_x),
         Sweep(1, ly, lx // 8, qy, wy, kept_y),
         Sweep(2, inner, 1, qz, wz, kept_z),
     ]
-    pltpu.make_async_copy(turned_y, turned_y, turn_sem).wait()
-
     @pl.when(is_root)
     def _():
         for axis in (0,):
@@ -265,9 +255,21 @@
         ],
         [halo(4, zsend.at[0], zh.at[0], 2, True), halo(5, zsend.at[1], zh.at[1], 2, False)],
     ]
-    for axis in (2, 1, 0):
-        for copy in halos[axis]:
-            copy.start()
+    for copy in halos[0]:
+        copy.start()
+    for c in range(5):
+        for g in range(groups):
+            turned = jnp.transpose(qx[c, pl.ds(x_edge + g * LANES, LANES), :])
+            for b in range(blocks):
+                qz[c, pl.ds(24 + b * groups + g, inner, stride=8), :] = turned[b * inner:(b + 1) * inner]
+            for k in range(3):
+                zsend[0, pl.ds((3 * c + k) * groups + g, 1), :] = turned[lz - 3 + k:lz - 2 + k]
+                zsend[1, pl.ds((3 * c + k) * groups + g, 1), :] = turned[k:k + 1]
+    for copy in halos[2]:
+        copy.start()
+    pltpu.make_async_copy(turned_y, turned_y, turn_sem).wait()
+    for copy in halos[1]:
+        copy.start()
 
     def fill_y():
         for copy in halos[1]:
@@ -374,10 +376,11 @@
         out[c, here, :] = acc[c, here, :] + value
 
     stores = []
-    chunk = lx // 4
+    ends = [0, (6 * lx) // 16, (11 * lx) // 16, (14 * lx) // 16, lx]
     for m in range(4):
-        sweep(0, rx, quarter, scale, kept, faces, place, 0 if m == 0 else m * chunk + 1, (m + 1) * chunk + 1, 2)
-        part = pl.ds(m * chunk * ly, chunk * ly)
+        low, high = ends[m], ends[m + 1]
+        sweep(0, rx, quarter, scale, kept, faces, place, 0 if m == 0 else low + 1, high + 1, 2)
+        part = pl.ds(low * ly, (high - low) * ly)
         stores.append(pltpu.make_async_copy(out.at[:, part, :], out_hbm.at[:, part, :], store_sem.at[m]))
         stores[-1].start()
     for store in stores:

time: 20 us -> 19.8 us (0.990)
  no operation moved by 1% of the time
where the time goes in v4:
time: 19.8 us; the launch traced here: 19.5 us
  Pallas kernels  19.5 us (98%)
    pallas_call x1, Pallas kernels, per_device(): pl.pallas_call(functools.partial(gather_kernel, sizes, cells, shape), nam...  16.3 us
    pallas_call x1, Pallas kernels, per_device(): pl.pallas_call(functools.partial(combine_kernel, shape), name='combine',...  3.14 us

profile of v4, /device:TPU:0, one launch (start us, length us, event | category | flops | bytes accessed | tf_op | source)
XLA Modules:
  0.0 19.5 jit_solution(2820081571572507082)
XLA Ops:
  0.0 16.3 %gather.1 = (f32[34,76,8,128]{3,2,1,0:T(8,128)S(1)}, f32[5,256,128]{2,1,0:T(8,128)S(1)}, f32[2,8,128]{2,1,0:T(8,128)S(1)}) custom-call(f32[5,16,16,128]{3,2,1,0:T(8,128)} %cons_hbm.1), custom_call_target="tpu_custom_call" | custom-call | tf_op jit(solution)/shard_map/gather/pallas_call | solution.py:413
  16.3 3.1 %combine.1 = f32[5,256,128]{2,1,0:T(8,128)} custom-call(f32[34,76,8,128]{3,2,1,0:T(8,128)S(1)} %get-tuple-element.8.kept, f32[5,256,128]{2,1,0:T(8,128)S(1)} %get-tuple-element.9.acc, f32[2,8,128]{2,1,0:T(8,128)S(1)} %get-tuple-element.10.factors), custom_call_target="tpu_custom_call" | custom-call | tf_op jit(solution)/shard_map/combine/pallas_call | solution.py:437
